TPU v7x, 32 devices: a whole 2x2x4 slice. The times are simulated.
32 devices in a mesh: freq: 8 (over z, y), rows: 4 (over x, core).
Axes of the slice: x: 2, y: 2, z: 4, core: 2. Of those that a mesh axis runs over, the one named last changes fastest.
Arguments:
- wavefield: bfloat16 [10240, 32, 1024], P('freq', 'rows'), may hold values from -6 to 6
- u_factors: bfloat16 [2, 16, 4, 256, 512], P(None, 'freq', 'rows'), may hold values from -0.25 to 0.25
- v_factors: bfloat16 [2, 16, 4, 512, 256], P(None, 'freq', 'rows'), may hold values from -0.375 to 0.375
- tile_ranks: int32 [16, 4, 40], P('freq', 'rows'), may hold values from 1 to 64, as said below
- tile_offsets: int32 [16, 4, 40], P('freq', 'rows'), may hold values from 0 to 511, as said below
Outputs:
- convolved: bfloat16 [1024, 32, 1024], P(('rows', 'freq'))
Inputs may be any that keep to these rules, and one draw needn't show every extreme that they name: tile_ranks[k, i, j] is the rank of tile (i, j) of frequency k; the ranks of one tile row sum to at most 512, exactly 512 on some row of every draw, and every tile row has a tile of rank 64. tile_offsets[k, i, j] is the sum of tile_ranks[k, i, j2] over j2 < j.
All inputs are finite; a program needn't handle non-finite values.
Results may differ from a plain program's by a relative error of at most 0.0072.
Values may be sent and summed in bfloat16 or wider, within the bound.
A program may use at most 128 MiB of HBM per device.

v0:
```python
import functools
import math

import jax
import jax.numpy as jnp
import numpy as np
from jax import lax
from jax.experimental import pallas as pl
from jax.experimental.pallas import tpu as pltpu
from jax.sharding import PartitionSpec as P

RANK_MAX = 64
MESH = pl.DeviceIdType.MESH
LANES = 128


def spectral_tables(freq_count, sample_count):
    freq_bins = jnp.arange(freq_count, dtype=jnp.int32) + 1
    sample_index = jnp.arange(sample_count, dtype=jnp.int32)
    phase_int = freq_bins[:, None] * sample_index[None, :] % sample_count
    angles = phase_int.astype(jnp.float32) * (2.0 * math.pi / sample_count)
    cosine = jnp.cos(angles)
    minus_sine = -jnp.sin(angles)
    stacked = jnp.stack([cosine, minus_sine], axis=1)
    forward = (stacked / math.sqrt(sample_count)).astype(jnp.bfloat16)
    inverse = (stacked / math.sqrt(freq_count)).astype(jnp.bfloat16)
    return (forward, inverse)


def tile_windows(v_row, u_row, starts, rank_max):
    columns = starts.shape[0]
    slot_index = (starts[:, None] + jnp.arange(rank_max, dtype=jnp.int32)[None, :]).reshape(-1)
    v_padded = jnp.pad(v_row, ((0, 0), (0, rank_max), (0, 0)))
    u_padded = jnp.pad(u_row, ((0, 0), (0, 0), (0, rank_max)))
    v_win = jnp.take(v_padded, slot_index, axis=1).reshape(2, columns, rank_max, v_row.shape[2])
    u_win = jnp.take(u_padded, slot_index, axis=2).reshape(2, u_row.shape[1], columns, rank_max)
    return (v_win, u_win)


def slot_lookup(starts, counts, rank_max, slot_count):
    position = jnp.arange(slot_count, dtype=jnp.int32)
    started = starts[:, None, :] <= position[None, :, None]
    owner_tile = jnp.sum(started.astype(jnp.int32), axis=2) - 1
    first_slot = jnp.max(jnp.where(started, starts[:, None, :], 0), axis=2)
    within = position[None, :] - first_slot
    live_slot = position[None, :] < (starts[:, -1] + counts[:, -1])[:, None]
    flat_index = jnp.where(live_slot, owner_tile * rank_max + within, 0)
    return (flat_index, live_slot)


def take_slots(values, chosen):
    return jnp.take(values, chosen, axis=1)


def general_device(wavefield, u_factors, v_factors, tile_ranks, tile_offsets):
    rec_dev, src_dev, samples = wavefield.shape
    freq_dev = u_factors.shape[1]
    rows_dev = u_factors.shape[2]
    tile_size = u_factors.shape[3]
    slot_count = u_factors.shape[4]
    freq_group = lax.axis_size("freq")
    row_group = lax.axis_size("rows")
    freqs = freq_dev * freq_group
    receivers = rec_dev * freq_group
    columns = receivers // tile_size
    sources = src_dev * row_group
    forward, inverse = spectral_tables(freqs, samples)
    spectrum = jnp.einsum("kct,rst->kcrs", forward, wavefield, preferred_element_type=jnp.float32)
    spectrum = spectrum.astype(jnp.bfloat16).reshape(freqs, 2, rec_dev * src_dev)
    windows = jax.vmap(
        functools.partial(tile_windows, rank_max=RANK_MAX), in_axes=(1, 1, 0), out_axes=(1, 1)
    )
    rank_slots = jnp.arange(RANK_MAX, dtype=jnp.int32)
    tile_row = 0
    v_win, u_win = windows(
        v_factors[:, :, tile_row], u_factors[:, :, tile_row], tile_offsets[:, tile_row]
    )
    rank_mask = rank_slots[None, None, :] < tile_ranks[:, tile_row, :, None]
    flat_index, live_slot = slot_lookup(
        tile_offsets[:, tile_row], tile_ranks[:, tile_row], RANK_MAX, slot_count
    )
    prepared = [(v_win, u_win, rank_mask, flat_index, live_slot)]
    by_frequency = lax.all_to_all(spectrum, "freq", split_axis=0, concat_axis=2, tiled=True)
    portion = lax.all_gather(by_frequency[None], "rows", axis=0, tiled=True)
    blocks_in = portion.shape[0]
    spectra = portion.reshape(blocks_in, freq_dev, 2, columns, tile_size, src_dev)
    spectra = jnp.transpose(spectra, (1, 2, 3, 4, 0, 5)).reshape(
        freq_dev, 2, columns, tile_size, blocks_in * src_dev
    )
    tile_row = 0
    v_win, u_win, rank_mask, flat_index, live_slot = prepared[tile_row]
    quadrants = jnp.einsum(
        "afjmr,fbjrs->fabjms", v_win, spectra, preferred_element_type=jnp.float32
    )
    coeffs = jnp.stack(
        [quadrants[:, 0, 0] - quadrants[:, 1, 1], quadrants[:, 0, 1] + quadrants[:, 1, 0]], axis=1
    )
    coeffs = jnp.where(rank_mask[:, None, :, :, None], coeffs, 0.0).astype(jnp.bfloat16)
    stacked = coeffs.reshape(freq_dev, 2, columns * RANK_MAX, blocks_in * src_dev)
    packed = jax.vmap(take_slots)(stacked, flat_index)
    packed = jnp.where(live_slot[:, None, :, None], packed, jnp.zeros((), jnp.bfloat16))
    products = jnp.einsum(
        "afrk,fcks->facrs", u_factors[:, :, tile_row], packed, preferred_element_type=jnp.float32
    )
    results = [
        jnp.stack(
            [products[:, 0, 0] - products[:, 1, 1], products[:, 0, 1] + products[:, 1, 0]], axis=1
        )
    ]
    merged = jnp.stack(results, axis=2)
    bands = merged.astype(jnp.bfloat16).reshape(
        freq_dev, 2, rows_dev * tile_size, blocks_in, src_dev
    )
    bands = bands.reshape(freq_dev, 2, rows_dev * tile_size * sources)
    returned = lax.all_to_all(bands, "freq", split_axis=2, concat_axis=0, tiled=True)
    series = jnp.einsum("kcq,kct->qt", returned, inverse, preferred_element_type=jnp.float32)
    return series.astype(jnp.bfloat16).reshape(rows_dev * tile_size // freq_group, sources, samples)


def host_tables(freq_count, sample_count):
    freq_bins = np.arange(freq_count) + 1
    phase = freq_bins[:, None] * np.arange(sample_count)[None, :] % sample_count
    angles = phase * (2.0 * math.pi / sample_count)
    stacked = np.stack([np.cos(angles), -np.sin(angles)], axis=1)
    stacked = stacked.reshape(2 * freq_count, sample_count)
    forward = (stacked / math.sqrt(sample_count)).astype(np.float32)
    inverse = (stacked / math.sqrt(freq_count)).astype(np.float32)
    return forward, inverse


def band_kernel(
    groups, chunks, tile, src_dev,
    wave, table, u_hbm, v_hbm, starts, counts, out_ref,
    u_ref, v_ref, wbuf, spec, send, xbuf, acc, bsend, brecv,
    usem, vsem, wsem, sa, ra, sx, rx, sp, rp, sq, rq, sb, rb,
):
    me = lax.axis_index("freq")
    row = lax.axis_index("rows")
    across = lax.rem(row + 2, 4)
    partner = row + 1 - 2 * lax.rem(row, 2)
    piece = send.shape[1] // groups
    freq_dev = u_ref.shape[1]
    slots = u_ref.shape[3]
    chunk_rows = tile * src_dev

    def load(c):
        return pltpu.make_async_copy(
            wave.at[pl.ds(c * chunk_rows, chunk_rows)], wbuf.at[c], wsem.at[c]
        )

    for c in range(chunks):
        load(c).start()
    load_v = pltpu.make_async_copy(v_hbm, v_ref, vsem)
    load_u = pltpu.make_async_copy(u_hbm, u_ref, usem)
    load_v.start()
    load_u.start()

    barrier = pltpu.get_barrier_semaphore()

    def greet(d, carry):
        peer = lax.rem(me + d, groups)
        pl.semaphore_signal(barrier, inc=1, device_id=(peer, row), device_id_type=MESH)
        return carry

    lax.fori_loop(1, groups, greet, 0)
    pl.semaphore_signal(barrier, inc=1, device_id=(me, across), device_id_type=MESH)
    pl.semaphore_signal(barrier, inc=1, device_id=(me, partner), device_id_type=MESH)
    pl.semaphore_wait(barrier, groups + 1)

    def exchange(c, peer, sender):
        return pltpu.make_async_remote_copy(
            src_ref=send.at[c, pl.ds(peer * piece, piece)],
            dst_ref=xbuf.at[c, sender, row],
            send_sem=sa.at[c, peer],
            recv_sem=ra.at[c, sender],
            device_id=(peer, row),
            device_id_type=MESH,
        )

    def forward(c, g, block, target, s_sem, r_sem):
        return pltpu.make_async_remote_copy(
            src_ref=xbuf.at[c, g, block],
            dst_ref=xbuf.at[c, g, block],
            send_sem=s_sem.at[c, g],
            recv_sem=r_sem.at[c, g],
            device_id=(me, target),
            device_id_type=MESH,
        )

    def to_across(c, g, block):
        return forward(c, g, block, across, sx, rx)

    def to_partner(c, g, block):
        return forward(c, g, block, partner, sp, rp)

    def to_partner_far(c, g, block):
        return forward(c, g, block, partner, sq, rq)

    acc[...] = jnp.zeros_like(acc)
    lane_mod = lax.rem(lax.broadcasted_iota(jnp.int32, (tile, LANES), 1), src_dev)
    sub = 2048

    def transform(c):
        load(c).wait()

        def block(b, carry):
            rows = pl.ds(pl.multiple_of(b * sub, sub), sub)
            values = lax.dot_general(
                wbuf[c, rows, :], table[...], (((1,), (0,)), ((), ())),
                preferred_element_type=jnp.float32,
            )
            for h in range(spec.shape[0]):
                spec[h, rows, :] = values[:, h * LANES : (h + 1) * LANES]
            return carry

        lax.fori_loop(0, chunk_rows // sub, block, 0)
        for h in range(spec.shape[0]):
            cols = slice(h * LANES, (h + 1) * LANES)
            picked = spec[h, pl.ds(0, tile, stride=src_dev), :]
            for s in range(1, src_dev):
                picked = jnp.where(
                    lane_mod == s, spec[h, pl.ds(s, tile, stride=src_dev), :], picked
                )
            send[c, cols, :] = picked.T.astype(jnp.bfloat16)
        own = pl.multiple_of(me * piece, piece)
        xbuf[c, me, row] = send[c, pl.ds(own, piece), :]

        def start(d, carry):
            exchange(c, lax.rem(me + d, groups), me).start()
            return carry

        lax.fori_loop(1, groups, start, 0)
        to_across(c, me, row).start()
        to_partner(c, me, row).start()

    def relay(c):
        def step(d, carry):
            g = lax.rem(me + groups - d, groups)
            exchange(c, g, g).wait_recv()
            to_across(c, g, row).start()
            to_partner(c, g, row).start()
            return carry

        lax.fori_loop(1, groups, step, 0)

    def relay_far(c):
        def step(d, carry):
            g = lax.rem(me + groups - d, groups)
            to_across(c, g, across).wait_recv()
            to_partner_far(c, g, across).start()
            return carry

        lax.fori_loop(0, groups, step, 0)

    def project(c):
        def arrive(d, carry):
            g = lax.rem(me + groups - d, groups)
            to_partner(c, g, partner).wait_recv()
            to_partner_far(c, g, lax.rem(partner + 2, 4)).wait_recv()
            return carry

        lax.fori_loop(0, groups, arrive, 0)
        slot = lax.broadcasted_iota(jnp.int32, (1, slots), 1)
        half = 2 * src_dev
        for k in range(freq_dev):
            left = xbuf[c, :, :, k * half : (k + 1) * half, :].reshape(groups * 4 * half, tile)
            for a in range(2):
                products = lax.dot_general(
                    left, v_ref[a, k], (((1,), (1,)), ((), ())),
                    preferred_element_type=jnp.float32,
                ).reshape(groups, 4 * half, slots)
                total = acc[k, a]
                for g in range(groups):
                    first = starts[k, g * chunks + c]
                    last = first + counts[k, g * chunks + c]
                    inside = (slot >= first) & (slot < last)
                    total = jnp.where(inside, products[g], total)
                acc[k, a] = total

    def step(c, carry):
        pl.when(c < chunks)(lambda: transform(c))
        pl.when((c >= 2) & (c < chunks + 2))(lambda: relay(c - 2))
        pl.when((c >= 3) & (c < chunks + 3))(lambda: relay_far(c - 3))
        pl.when(c == 4)(load_v.wait)
        pl.when(c >= 4)(lambda: project(c - 4))
        return carry

    lax.fori_loop(0, chunks + 4, step, 0)

    load_u.wait()
    rows_out = []
    contract = (((1,), (1,)), ((), ()))
    sources = 4 * src_dev
    q_low = LANES // sources
    q_high = tile // groups // q_low
    for k in range(freq_dev):
        first = acc[k, 0].reshape(4, 2, src_dev, slots)
        second = acc[k, 1].reshape(4, 2, src_dev, slots)
        real = (first[:, 0] - second[:, 1]).reshape(sources, slots)
        imag = (first[:, 1] + second[:, 0]).reshape(sources, slots)
        straight = jnp.concatenate([real, imag], axis=0).astype(jnp.bfloat16)
        turned = jnp.concatenate([-imag, real], axis=0).astype(jnp.bfloat16)
        band = lax.dot_general(u_ref[0, k], straight, contract, preferred_element_type=jnp.float32)
        band = band + lax.dot_general(
            u_ref[1, k], turned, contract, preferred_element_type=jnp.float32
        )
        split = band.reshape(groups, q_low, q_high, 2 * sources)
        for part in range(2):
            lanes = slice(part * sources, (part + 1) * sources)
            rows_out.append(
                jnp.concatenate([split[:, q, :, lanes] for q in range(q_low)], axis=-1)
            )
    bsend[...] = jnp.concatenate(rows_out, axis=1).astype(jnp.bfloat16)

    def give_back(peer, sender):
        return pltpu.make_async_remote_copy(
            src_ref=bsend.at[peer],
            dst_ref=brecv.at[sender],
            send_sem=sb.at[peer],
            recv_sem=rb.at[sender],
            device_id=(peer, row),
            device_id_type=MESH,
        )

    def start_back(d, carry):
        give_back(lax.rem(me + d, groups), me).start()
        return carry

    lax.fori_loop(1, groups, start_back, 0)
    brecv[me] = bsend[me]

    def drain(c, carry):
        def one(d, inner):
            g = lax.rem(me + d, groups)
            pl.when(d > 0)(lambda: exchange(c, g, me).wait_send())
            to_across(c, g, row).wait_send()
            to_partner(c, g, row).wait_send()
            to_partner_far(c, g, across).wait_send()
            return inner

        return lax.fori_loop(0, groups, one, carry)

    lax.fori_loop(0, chunks, drain, 0)

    def finish(d, carry):
        peer = lax.rem(me + d, groups)
        give_back(peer, me).wait_send()
        source = lax.rem(me + groups - d, groups)
        give_back(source, source).wait_recv()
        return carry

    lax.fori_loop(1, groups, finish, 0)
    out_ref[...] = brecv[...].reshape(out_ref.shape)


def series_kernel(q_high, band_ref, table_ref, out_ref, wide):
    step = pl.program_id(0)

    @pl.when(step == 0)
    def _():
        wide[...] = band_ref[...].astype(jnp.float32)

    q_low, q_step, sources, samples = out_ref.shape
    for q in range(q_step):
        rows = pl.ds(step * q_step + q, band_ref.shape[0] // q_high, stride=q_high)
        series = jnp.dot(
            wide[rows, :].T.astype(jnp.bfloat16), table_ref[...],
            preferred_element_type=jnp.float32,
        )
        out_ref[:, q] = series.astype(jnp.bfloat16).reshape(q_low, sources, samples)


def fast_device(wavefield, u_factors, v_factors, tile_ranks, tile_offsets):
    rec_dev, src_dev, samples = wavefield.shape
    freq_dev, tile, slots = u_factors.shape[1], u_factors.shape[3], u_factors.shape[4]
    groups = lax.axis_size("freq")
    chunks = rec_dev // tile
    forward, inverse = host_tables(freq_dev * groups, samples)
    table = jnp.asarray(np.repeat(forward.T, src_dev, axis=1)).astype(jnp.bfloat16)
    inverse = jnp.asarray(inverse).astype(jnp.bfloat16)
    columns = table.shape[1]
    piece = columns // groups
    sources = 4 * src_dev
    q_dev = tile // groups
    q_low = LANES // sources
    q_high = q_dev // q_low
    q_step = q_high // math.gcd(q_high, 2)
    band_rows = 2 * freq_dev * q_high
    vmem = pl.BlockSpec(memory_space=pltpu.VMEM)
    hbm = pl.BlockSpec(memory_space=pl.ANY)
    smem = pl.BlockSpec(memory_space=pltpu.SMEM)
    dma = pltpu.SemaphoreType.DMA
    bands = pl.pallas_call(
        functools.partial(band_kernel, groups, chunks, tile, src_dev),
        out_shape=jax.ShapeDtypeStruct((groups * band_rows, LANES), jnp.bfloat16),
        in_specs=[hbm, vmem, hbm, hbm, smem, smem],
        out_specs=vmem,
        scratch_shapes=[
            pltpu.VMEM((2, freq_dev, tile, slots), jnp.bfloat16),
            pltpu.VMEM((2, freq_dev, slots, tile), jnp.bfloat16),
            pltpu.VMEM((chunks, tile * src_dev, samples), jnp.bfloat16),
            pltpu.VMEM((columns // LANES, tile * src_dev, LANES), jnp.float32),
            pltpu.VMEM((chunks, columns, tile), jnp.bfloat16),
            pltpu.VMEM((chunks, groups, 4, piece, tile), jnp.bfloat16),
            pltpu.VMEM((freq_dev, 2, 8 * src_dev, slots), jnp.float32),
            pltpu.VMEM((groups, band_rows, LANES), jnp.bfloat16),
            pltpu.VMEM((groups, band_rows, LANES), jnp.bfloat16),
            dma,
            dma,
            dma((chunks,)),
        ]
        + [dma((chunks, groups)) for _ in range(8)]
        + [dma((groups,)), dma((groups,))],
        compiler_params=pltpu.CompilerParams(
            collective_id=0, has_side_effects=True, vmem_limit_bytes=60 * 1024 * 1024
        ),
        name="bands",
    )(
        wavefield.reshape(rec_dev * src_dev, samples),
        table,
        u_factors[:, :, 0],
        v_factors[:, :, 0],
        tile_offsets[:, 0],
        tile_ranks[:, 0],
    )
    series = pl.pallas_call(
        functools.partial(series_kernel, q_high),
        grid=(q_high // q_step,),
        out_shape=jax.ShapeDtypeStruct((q_low, q_high, sources, samples), jnp.bfloat16),
        in_specs=[
            pl.BlockSpec(bands.shape, lambda q: (0, 0)),
            pl.BlockSpec(inverse.shape, lambda q: (0, 0)),
        ],
        out_specs=pl.BlockSpec((q_low, q_step, sources, samples), lambda q: (0, q, 0, 0)),
        scratch_shapes=[pltpu.VMEM(bands.shape, jnp.float32)],
        name="series",
    )(bands, inverse)
    return series.reshape(q_dev, sources, samples)


def per_device(wavefield, u_factors, v_factors, tile_ranks, tile_offsets):
    rec_dev, src_dev, samples = wavefield.shape
    tile, slots = u_factors.shape[3], u_factors.shape[4]
    groups = lax.axis_size("freq")
    aligned = tile % LANES == 0 and rec_dev % tile == 0 and slots % LANES == 0
    aligned = aligned and samples % LANES == 0
    counts = u_factors.shape[1] == 2 and u_factors.shape[2] == 1 and src_dev == 8
    counts = counts and lax.axis_size("rows") == 4 and groups > 1 and groups * 32 % LANES == 0
    if aligned and counts and tile == groups * 32:
        return fast_device(wavefield, u_factors, v_factors, tile_ranks, tile_offsets)
    return general_device(wavefield, u_factors, v_factors, tile_ranks, tile_offsets)


def solution(mesh):
    placed = (
        P("freq", "rows", None),
        P(None, "freq", "rows", None, None),
        P(None, "freq", "rows", None, None),
        P("freq", "rows", None),
        P("freq", "rows", None),
    )
    return jax.shard_map(
        per_device,
        mesh=mesh,
        in_specs=placed,
        out_specs=P(("rows", "freq"), None, None),
        check_vma=False,
    )
```

profile of v0, /device:TPU:0, one launch (start us, length us, event | category | flops | bytes accessed | tf_op | source)
XLA Modules:
  0.0 43.1 jit_solution(5796317490827979005)
XLA Ops:
  0.0 40.3 %bands.1.band_ref = bf16[256,128]{1,0:T(8,128)(2,1)} custom-call(bf16[10240,1024]{1,0:T(8,128)(2,1)} %bitcast.6, bf16[1024,256]{1,0:T(8,128)(2,1)} %constant.10.table, bf16[2,2,256,512]{3,2,1,0:T(8,128)(2,1)} %bitcast.7, bf16[2,2,512,256]{3,2,1,0:T(8,128)(2,1)} %bitcast.8, s32[2,40]{1,0:T(2,128)} %bitcast.9, s32[2,40]{1,0:T(2,128)} %bitcast.10), custom_call_target="tpu_custom_call" | custom-call | tf_op jit(solution)/shard_map/bands/pallas_call | solution.py:393
  40.3 2.9 %series.1 = bf16[4,8,32,1024]{3,2,1,0:T(8,128)(2,1)} custom-call(bf16[256,128]{1,0:T(8,128)(2,1)} %bands.1.band_ref, bf16[32,1024]{1,0:T(8,128)(2,1)} %constant.11.table_ref), custom_call_target="tpu_custom_call" | custom-call | tf_op jit(solution)/shard_map/series/pallas_call | solution.py:426
where the time goes:
time: 43.3 us; the launch traced here: 43.1 us
  Pallas kernels  43.1 us (100%)
    pallas_call x1, Pallas kernels, fast_device(): pl.pallas_call(functools.partial(band_kernel, groups, chunks, tile, src_d...  40.3 us
    pallas_call x1, Pallas kernels, fast_device(): pl.pallas_call(functools.partial(series_kernel, q_high), grid=(q_high //...  2.86 us

commit v1 on v0

v1 whole, which is shorter than its diff:
```python
import functools
import math

import jax
import jax.numpy as jnp
import numpy as np
from jax import lax
from jax.experimental import pallas as pl
from jax.experimental.pallas import tpu as pltpu
from jax.sharding import PartitionSpec as P

RANK_MAX = 64
MESH = pl.DeviceIdType.MESH
LANES = 128
LAG = 3


def spectral_tables(freq_count, sample_count):
    freq_bins = jnp.arange(freq_count, dtype=jnp.int32) + 1
    sample_index = jnp.arange(sample_count, dtype=jnp.int32)
    phase_int = freq_bins[:, None] * sample_index[None, :] % sample_count
    angles = phase_int.astype(jnp.float32) * (2.0 * math.pi / sample_count)
    cosine = jnp.cos(angles)
    minus_sine = -jnp.sin(angles)
    stacked = jnp.stack([cosine, minus_sine], axis=1)
    forward = (stacked / math.sqrt(sample_count)).astype(jnp.bfloat16)
    inverse = (stacked / math.sqrt(freq_count)).astype(jnp.bfloat16)
    return (forward, inverse)


def tile_windows(v_row, u_row, starts, rank_max):
    columns = starts.shape[0]
    slot_index = (starts[:, None] + jnp.arange(rank_max, dtype=jnp.int32)[None, :]).reshape(-1)
    v_padded = jnp.pad(v_row, ((0, 0), (0, rank_max), (0, 0)))
    u_padded = jnp.pad(u_row, ((0, 0), (0, 0), (0, rank_max)))
    v_win = jnp.take(v_padded, slot_index, axis=1).reshape(2, columns, rank_max, v_row.shape[2])
    u_win = jnp.take(u_padded, slot_index, axis=2).reshape(2, u_row.shape[1], columns, rank_max)
    return (v_win, u_win)


def slot_lookup(starts, counts, rank_max, slot_count):
    position = jnp.arange(slot_count, dtype=jnp.int32)
    started = starts[:, None, :] <= position[None, :, None]
    owner_tile = jnp.sum(started.astype(jnp.int32), axis=2) - 1
    first_slot = jnp.max(jnp.where(started, starts[:, None, :], 0), axis=2)
    within = position[None, :] - first_slot
    live_slot = position[None, :] < (starts[:, -1] + counts[:, -1])[:, None]
    flat_index = jnp.where(live_slot, owner_tile * rank_max + within, 0)
    return (flat_index, live_slot)


def take_slots(values, chosen):
    return jnp.take(values, chosen, axis=1)


def general_device(wavefield, u_factors, v_factors, tile_ranks, tile_offsets):
    rec_dev, src_dev, samples = wavefield.shape
    freq_dev = u_factors.shape[1]
    rows_dev = u_factors.shape[2]
    tile_size = u_factors.shape[3]
    slot_count = u_factors.shape[4]
    freq_group = lax.axis_size("freq")
    row_group = lax.axis_size("rows")
    freqs = freq_dev * freq_group
    receivers = rec_dev * freq_group
    columns = receivers // tile_size
    sources = src_dev * row_group
    forward, inverse = spectral_tables(freqs, samples)
    spectrum = jnp.einsum("kct,rst->kcrs", forward, wavefield, preferred_element_type=jnp.float32)
    spectrum = spectrum.astype(jnp.bfloat16).reshape(freqs, 2, rec_dev * src_dev)
    windows = jax.vmap(
        functools.partial(tile_windows, rank_max=RANK_MAX), in_axes=(1, 1, 0), out_axes=(1, 1)
    )
    rank_slots = jnp.arange(RANK_MAX, dtype=jnp.int32)
    tile_row = 0
    v_win, u_win = windows(
        v_factors[:, :, tile_row], u_factors[:, :, tile_row], tile_offsets[:, tile_row]
    )
    rank_mask = rank_slots[None, None, :] < tile_ranks[:, tile_row, :, None]
    flat_index, live_slot = slot_lookup(
        tile_offsets[:, tile_row], tile_ranks[:, tile_row], RANK_MAX, slot_count
    )
    prepared = [(v_win, u_win, rank_mask, flat_index, live_slot)]
    by_frequency = lax.all_to_all(spectrum, "freq", split_axis=0, concat_axis=2, tiled=True)
    portion = lax.all_gather(by_frequency[None], "rows", axis=0, tiled=True)
    blocks_in = portion.shape[0]
    spectra = portion.reshape(blocks_in, freq_dev, 2, columns, tile_size, src_dev)
    spectra = jnp.transpose(spectra, (1, 2, 3, 4, 0, 5)).reshape(
        freq_dev, 2, columns, tile_size, blocks_in * src_dev
    )
    tile_row = 0
    v_win, u_win, rank_mask, flat_index, live_slot = prepared[tile_row]
    quadrants = jnp.einsum(
        "afjmr,fbjrs->fabjms", v_win, spectra, preferred_element_type=jnp.float32
    )
    coeffs = jnp.stack(
        [quadrants[:, 0, 0] - quadrants[:, 1, 1], quadrants[:, 0, 1] + quadrants[:, 1, 0]], axis=1
    )
    coeffs = jnp.where(rank_mask[:, None, :, :, None], coeffs, 0.0).astype(jnp.bfloat16)
    stacked = coeffs.reshape(freq_dev, 2, columns * RANK_MAX, blocks_in * src_dev)
    packed = jax.vmap(take_slots)(stacked, flat_index)
    packed = jnp.where(live_slot[:, None, :, None], packed, jnp.zeros((), jnp.bfloat16))
    products = jnp.einsum(
        "afrk,fcks->facrs", u_factors[:, :, tile_row], packed, preferred_element_type=jnp.float32
    )
    results = [
        jnp.stack(
            [products[:, 0, 0] - products[:, 1, 1], products[:, 0, 1] + products[:, 1, 0]], axis=1
        )
    ]
    merged = jnp.stack(results, axis=2)
    bands = merged.astype(jnp.bfloat16).reshape(
        freq_dev, 2, rows_dev * tile_size, blocks_in, src_dev
    )
    bands = bands.reshape(freq_dev, 2, rows_dev * tile_size * sources)
    returned = lax.all_to_all(bands, "freq", split_axis=2, concat_axis=0, tiled=True)
    series = jnp.einsum("kcq,kct->qt", returned, inverse, preferred_element_type=jnp.float32)
    return series.astype(jnp.bfloat16).reshape(rows_dev * tile_size // freq_group, sources, samples)


def host_tables(freq_count, sample_count):
    freq_bins = np.arange(freq_count) + 1
    phase = freq_bins[:, None] * np.arange(sample_count)[None, :] % sample_count
    angles = phase * (2.0 * math.pi / sample_count)
    stacked = np.stack([np.cos(angles), -np.sin(angles)], axis=1)
    stacked = stacked.reshape(2 * freq_count, sample_count)
    forward = (stacked / math.sqrt(sample_count)).astype(np.float32)
    inverse = (stacked / math.sqrt(freq_count)).astype(np.float32)
    return forward, inverse


def band_kernel(
    groups, chunks, tile, src_dev,
    wave, table_hbm, u_hbm, v_hbm, starts_hbm, counts_hbm, out_ref,
    starts, counts, table, u_ref, v_ref, owner, wbuf, spec, send, xbuf, acc, bsend, brecv,
    isem, tsem, usem, vsem, wsem, sa, ra, sx, rx, sf, rv, ru, ro, sb, rb,
):
    me = lax.axis_index("freq")
    row = lax.axis_index("rows")
    core = lax.rem(row, 2)
    side = row // 2
    across = lax.rem(row + 2, 4)
    partner = row + 1 - 2 * core
    half = groups // 2
    own_half = me // half
    steps = 2 * chunks
    width = tile // 2
    freq_dev = owner.shape[1]
    slots = owner.shape[3]
    piece = send.shape[1] // groups
    factors = u_ref.shape[1]
    step_rows = width * src_dev

    def load(h):
        return pltpu.make_async_copy(
            wave.at[pl.ds(h * step_rows, step_rows)], wbuf.at[h], wsem.at[h]
        )

    load_table = pltpu.make_async_copy(table_hbm, table, tsem)
    load_v = pltpu.make_async_copy(v_hbm, v_ref.at[0], vsem)
    load_u = pltpu.make_async_copy(u_hbm, u_ref.at[0], usem)
    load_starts = pltpu.make_async_copy(starts_hbm, starts, isem.at[0])
    load_counts = pltpu.make_async_copy(counts_hbm, counts, isem.at[1])
    load(0).start()
    load_table.start()
    load_starts.start()
    load_counts.start()

    barrier = pltpu.get_barrier_semaphore()

    def greet(d, carry):
        peer = lax.rem(me + d, groups)
        pl.semaphore_signal(barrier, inc=1, device_id=(peer, row), device_id_type=MESH)
        pl.semaphore_signal(barrier, inc=1, device_id=(peer, partner), device_id_type=MESH)
        return carry

    lax.fori_loop(1, groups, greet, 0)
    pl.semaphore_signal(barrier, inc=1, device_id=(me, across), device_id_type=MESH)
    pl.semaphore_signal(barrier, inc=1, device_id=(me, partner), device_id_type=MESH)

    def start_load(h, carry):
        load(h).start()
        return carry

    lax.fori_loop(1, steps, start_load, 0)
    load_v.start()
    load_u.start()

    load_starts.wait()
    load_counts.wait()
    slot = lax.broadcasted_iota(jnp.int32, (8, slots), 1)
    for k in range(freq_dev):
        tiles = groups * chunks

        def count_started(j, held):
            return held + (slot >= starts[k, j]).astype(jnp.int32)

        held = lax.fori_loop(0, tiles, count_started, jnp.full((8, slots), -1, jnp.int32), unroll=8)
        live = slot < starts[k, tiles - 1] + counts[k, tiles - 1]
        owner[0, k] = jnp.where(live, held, -1)
    acc[...] = jnp.zeros_like(acc)
    lane_mod = lax.rem(lax.broadcasted_iota(jnp.int32, (width, LANES), 1), src_dev)

    def exchange(h, peer, sender, r_sem):
        return pltpu.make_async_remote_copy(
            src_ref=send.at[h, pl.ds(peer * piece, piece)],
            dst_ref=xbuf.at[h, side, sender],
            send_sem=sa,
            recv_sem=r_sem,
            device_id=(peer, row),
            device_id_type=MESH,
        )

    def cross(h, first, count, block):
        return pltpu.make_async_remote_copy(
            src_ref=xbuf.at[h, block, pl.ds(first, count)],
            dst_ref=xbuf.at[h, block, pl.ds(first, count)],
            send_sem=sx,
            recv_sem=rx.at[h],
            device_id=(me, across),
            device_id_type=MESH,
        )

    def to_partner(src, dst, r_sem):
        return pltpu.make_async_remote_copy(
            src_ref=src,
            dst_ref=dst,
            send_sem=sf,
            recv_sem=r_sem,
            device_id=(me, partner),
            device_id_type=MESH,
        )

    def share_v(n):
        return to_partner(v_hbm.at[n], v_ref.at[1, n], rv)

    def share_u(n):
        return to_partner(u_hbm.at[n], u_ref.at[1, n], ru)

    share_owner = to_partner(owner.at[0], owner.at[1], ro)

    def transform(h):
        load(h).wait()
        values = lax.dot_general(
            wbuf[h], table[...], (((1,), (0,)), ((), ())),
            preferred_element_type=jnp.float32,
        )
        for p in range(spec.shape[0]):
            spec[p] = values[:, p * LANES : (p + 1) * LANES]
        for p in range(spec.shape[0]):
            cols = slice(p * LANES, (p + 1) * LANES)
            picked = spec[p, pl.ds(0, width, stride=src_dev), :]
            for s in range(1, src_dev):
                picked = jnp.where(
                    lane_mod == s, spec[p, pl.ds(s, width, stride=src_dev), :], picked
                )
            send[h, cols, :] = picked.T.astype(jnp.bfloat16)
        own = pl.multiple_of(me * piece, piece)
        xbuf[h, side, me] = send[h, pl.ds(own, piece), :]

    def distribute(h):
        cross(h, me, 1, side).start()
        for d in range(1, half):
            peer = own_half * half + lax.rem(me + d, half)
            exchange(h, peer, me, ra.at[h, 0]).start()
        for d in range(half):
            peer = (1 - own_half) * half + lax.rem(me + d, half)
            exchange(h, peer, me, ra.at[h, 1]).start()

    def relay_near(h):
        pltpu.make_async_copy(
            xbuf.at[h, side, pl.ds(0, half - 1)], xbuf.at[h, side, pl.ds(0, half - 1)], ra.at[h, 0]
        ).wait()
        for d in range(1, half):
            cross(h, own_half * half + lax.rem(me + d, half), 1, side).start()

    def relay_far(h):
        pltpu.make_async_copy(
            xbuf.at[h, side, pl.ds(0, half)], xbuf.at[h, side, pl.ds(0, half)], ra.at[h, 1]
        ).wait()
        cross(h, (1 - own_half) * half, half, side).start()

    def project(c):
        for n in range(2):
            cross(2 * c + n, 0, groups, 1 - side).wait_recv()
        rows = 2 * src_dev
        for k in range(freq_dev):
            parts = [
                xbuf[2 * c + n, :, :, k * rows : (k + 1) * rows, :].reshape(2 * groups * rows, width)
                for n in range(2)
            ]
            left = jnp.concatenate(parts, axis=1)
            for i in range(2):
                held = owner[i, k]
                inside = [(held == g * chunks + c)[0:1] for g in range(groups)]
                for a in range(2):
                    products = lax.dot_general(
                        left, v_ref[i, a * freq_dev + k], (((1,), (1,)), ((), ())),
                        preferred_element_type=jnp.float32,
                    ).reshape(2, groups, rows, slots)
                    total = acc[i, k, a]
                    for g in range(groups):
                        total = jnp.where(inside[g][None], products[:, g], total)
                    acc[i, k, a] = total

    def first_pass(h, carry):
        transform(h)
        pl.when(h == 0)(lambda: pl.semaphore_wait(barrier, 2 * groups))
        distribute(h)
        pl.when(h == 1)(share_owner.start)
        pl.when((h >= 2) & (h < 2 + factors))(lambda: share_v(h - 2).start())
        pl.when((h >= 2 + factors) & (h < 2 + 2 * factors))(lambda: share_u(h - 2 - factors).start())
        pl.when(h >= LAG)(lambda: relay_near(h - LAG))
        pl.when(h == LAG + 2)(lambda: relay_far(0))
        pl.when(h > 2 * LAG)(lambda: relay_far(h - 2 * LAG))
        return carry

    load_table.wait()
    lax.fori_loop(0, steps, first_pass, 0)
    load_v.wait()
    to_partner(v_ref.at[0], v_ref.at[1], rv).wait_recv()
    share_owner.wait_recv()

    near_turn = {steps - LAG + n: n for n in range(LAG)}
    far_turn = {}
    for c in range(chunks):
        for h in range(steps - 2 * LAG, min(steps, max(2 * c + 4, steps + 1 - 2 * LAG + c))):
            far_turn.setdefault(h, c)

    def second_pass(c, carry):
        for h, turn in far_turn.items():
            pl.when(c == turn)(functools.partial(relay_far, h))
        for h, turn in near_turn.items():
            pl.when(c == turn)(functools.partial(relay_near, h))
        project(c)
        return carry

    lax.fori_loop(0, chunks, second_pass, 0)

    load_u.wait()
    to_partner(u_ref.at[0], u_ref.at[1], ru).wait_recv()

    def give_back(i, peer):
        return pltpu.make_async_remote_copy(
            src_ref=bsend.at[i, peer],
            dst_ref=brecv.at[core * groups + me],
            send_sem=sb,
            recv_sem=rb,
            device_id=(peer, partner if i else row),
            device_id_type=MESH,
        )

    contract = (((1,), (1,)), ((), ()))
    sources = 2 * src_dev
    q_low = LANES // (2 * sources)
    q_high = tile // groups // q_low
    for i in (1, 0):
        rows_out = []
        for k in range(freq_dev):
            first = acc[i, k, 0].reshape(2, 2, src_dev, slots)
            second = acc[i, k, 1].reshape(2, 2, src_dev, slots)
            real = (first[:, 0] - second[:, 1]).reshape(sources, slots)
            imag = (first[:, 1] + second[:, 0]).reshape(sources, slots)
            straight = jnp.concatenate([real, imag], axis=0).astype(jnp.bfloat16)
            turned = jnp.concatenate([-imag, real], axis=0).astype(jnp.bfloat16)
            band = lax.dot_general(
                u_ref[i, k], straight, contract, preferred_element_type=jnp.float32
            )
            band = band + lax.dot_general(
                u_ref[i, freq_dev + k], turned, contract, preferred_element_type=jnp.float32
            )
            split = band.reshape(groups, q_low, q_high, 2 * sources)
            rows_out.append(jnp.concatenate([split[:, q] for q in range(q_low)], axis=-1))
        bsend[i] = jnp.concatenate(rows_out, axis=1).astype(jnp.bfloat16)

    def start_back(d, carry):
        give_back(1, lax.rem(me + groups // 2 + d, groups)).start()
        pl.when(d != groups // 2)(lambda: give_back(0, lax.rem(me + groups // 2 + d, groups)).start())
        return carry

    lax.fori_loop(0, groups, start_back, 0)
    brecv[core * groups + me] = bsend[0, me]

    sent = send.at[:, pl.ds(0, (groups - 1) * piece)]
    pltpu.make_async_copy(sent, sent, sa).wait()
    pltpu.make_async_copy(xbuf.at[:, 0], xbuf.at[:, 0], sx).wait()
    pltpu.make_async_copy(v_ref.at[0], v_ref.at[0], sf).wait()
    pltpu.make_async_copy(u_ref.at[0], u_ref.at[0], sf).wait()
    pltpu.make_async_copy(owner.at[0], owner.at[0], sf).wait()
    arrived = brecv.at[pl.ds(0, 2 * groups - 1)]
    pltpu.make_async_copy(arrived, arrived, sb).wait()
    pltpu.make_async_copy(arrived, arrived, rb).wait()
    out_ref[...] = brecv[...].reshape(out_ref.shape)


def series_kernel(band_ref, table_ref, out_hbm, wide, out, sem):
    q_low, q_high, sources, samples = out.shape
    block = band_ref.shape[0] // 2
    half = sources // 2
    low = band_ref[:block, :].astype(jnp.float32)
    high = band_ref[block:, :].astype(jnp.float32)
    first = lax.broadcasted_iota(jnp.int32, low.shape, 1) % sources < half
    wide[0] = jnp.where(first, low, pltpu.roll(high, half, 1))
    wide[1] = jnp.where(first, pltpu.roll(low, LANES - half, 1), high)

    for q in range(q_high):
        rows = pl.ds(q, block // q_high, stride=q_high)
        left = jnp.concatenate([wide[0, rows, :], wide[1, rows, :]], axis=0).T
        left = left.reshape(q_low, 2, 2, half // 2, left.shape[1])
        left = jnp.swapaxes(left, 1, 2).reshape(q_low * sources, left.shape[-1])
        series = jnp.dot(
            left.astype(jnp.bfloat16), table_ref[...], preferred_element_type=jnp.float32
        )
        out[:, q] = series.astype(jnp.bfloat16).reshape(q_low, sources, samples)
        pltpu.make_async_copy(out.at[:, q], out_hbm.at[:, q], sem).start()
    pltpu.make_async_copy(out, out_hbm, sem).wait()


def fast_device(wavefield, u_factors, v_factors, tile_ranks, tile_offsets):
    rec_dev, src_dev, samples = wavefield.shape
    freq_dev, tile, slots = u_factors.shape[1], u_factors.shape[3], u_factors.shape[4]
    groups = lax.axis_size("freq")
    chunks = rec_dev // tile
    steps, width = 2 * chunks, tile // 2
    freqs = freq_dev * groups
    forward, inverse = host_tables(freqs, samples)
    table = jnp.asarray(np.repeat(forward.T, src_dev, axis=1)).astype(jnp.bfloat16)
    inverse = inverse.reshape(freqs, 2, samples).transpose(1, 0, 2).reshape(2 * freqs, samples)
    inverse = jnp.asarray(inverse).astype(jnp.bfloat16)
    columns = table.shape[1]
    piece = columns // groups
    sources = 4 * src_dev
    q_dev = tile // groups
    q_low = LANES // sources
    q_high = q_dev // q_low
    band_rows = freq_dev * q_high
    factors = 2 * freq_dev
    vmem = pl.BlockSpec(memory_space=pltpu.VMEM)
    hbm = pl.BlockSpec(memory_space=pl.ANY)
    dma = pltpu.SemaphoreType.DMA
    bands = pl.pallas_call(
        functools.partial(band_kernel, groups, chunks, tile, src_dev),
        out_shape=jax.ShapeDtypeStruct((2 * groups * band_rows, LANES), jnp.bfloat16),
        in_specs=[hbm] * 6,
        out_specs=vmem,
        scratch_shapes=[
            pltpu.SMEM(tile_offsets[:, 0].shape, jnp.int32),
            pltpu.SMEM(tile_ranks[:, 0].shape, jnp.int32),
            pltpu.VMEM((samples, columns), jnp.bfloat16),
            pltpu.VMEM((2, factors, tile, slots), jnp.bfloat16),
            pltpu.VMEM((2, factors, slots, tile), jnp.bfloat16),
            pltpu.VMEM((2, freq_dev, 8, slots), jnp.int32),
            pltpu.VMEM((steps, width * src_dev, samples), jnp.bfloat16),
            pltpu.VMEM((columns // LANES, width * src_dev, LANES), jnp.float32),
            pltpu.VMEM((steps, columns, width), jnp.bfloat16),
            pltpu.VMEM((steps, 2, groups, piece, width), jnp.bfloat16),
            pltpu.VMEM((2, freq_dev, 2, 2, 2 * src_dev, slots), jnp.float32),
            pltpu.VMEM((2, groups, band_rows, LANES), jnp.bfloat16),
            pltpu.VMEM((2 * groups, band_rows, LANES), jnp.bfloat16),
            dma((2,)), dma, dma, dma, dma((steps,)),
            dma, dma((steps, 2)), dma, dma((steps,)),
            dma, dma, dma, dma, dma, dma,
        ],
        compiler_params=pltpu.CompilerParams(
            collective_id=0, has_side_effects=True, vmem_limit_bytes=60 * 1024 * 1024
        ),
        name="bands",
    )(
        wavefield.reshape(rec_dev * src_dev, samples),
        table,
        u_factors.reshape(factors, tile, slots),
        v_factors.reshape(factors, slots, tile),
        tile_offsets[:, 0],
        tile_ranks[:, 0],
    )
    shape = (q_low, q_high, sources, samples)
    series = pl.pallas_call(
        series_kernel,
        out_shape=jax.ShapeDtypeStruct(shape, jnp.bfloat16),
        in_specs=[vmem, vmem],
        out_specs=hbm,
        scratch_shapes=[
            pltpu.VMEM((2, bands.shape[0] // 2, LANES), jnp.float32),
            pltpu.VMEM(shape, jnp.bfloat16),
            dma,
        ],
        name="series",
    )(bands, inverse)
    return series.reshape(q_dev, sources, samples)


def per_device(wavefield, u_factors, v_factors, tile_ranks, tile_offsets):
    rec_dev, src_dev, samples = wavefield.shape
    tile, slots = u_factors.shape[3], u_factors.shape[4]
    groups = lax.axis_size("freq")
    aligned = tile % LANES == 0 and rec_dev % tile == 0 and slots % LANES == 0
    aligned = aligned and samples % LANES == 0
    counts = u_factors.shape[1] == 2 and u_factors.shape[2] == 1 and src_dev == 8
    counts = counts and lax.axis_size("rows") == 4 and groups % 2 == 0
    if aligned and counts and tile == groups * 32:
        return fast_device(wavefield, u_factors, v_factors, tile_ranks, tile_offsets)
    return general_device(wavefield, u_factors, v_factors, tile_ranks, tile_offsets)


def solution(mesh):
    placed = (
        P("freq", "rows", None),
        P(None, "freq", "rows", None, None),
        P(None, "freq", "rows", None, None),
        P("freq", "rows", None),
        P("freq", "rows", None),
    )
    return jax.shard_map(
        per_device,
        mesh=mesh,
        in_specs=placed,
        out_specs=P(("rows", "freq"), None, None),
        check_vma=False,
    )
```

time: 43.3 us -> 36.3 us (0.84)
  Pallas kernels: 43.1 us -> 36.2 us
    pallas_call x1, Pallas kernels: 40.3 us -> 33.6 us  [fast_device(): pl.pallas_call(functools.partial(band_kernel, groups, chunks, tile, src_d...]
where the time goes in v1:
time: 36.3 us; the launch traced here: 36.2 us
  Pallas kernels  36.2 us (100%)
    pallas_call x1, Pallas kernels, fast_device(): pl.pallas_call(functools.partial(band_kernel, groups, chunks, tile, src_d...  33.6 us
    pallas_call x1, Pallas kernels, fast_device(): pl.pallas_call(series_kernel, out_shape=jax.ShapeDtypeStruct(shape, jnp.b...  2.56 us

profile of v1, /device:TPU:0, one launch (start us, length us, event | category | flops | bytes accessed | tf_op | source)
XLA Modules:
  0.0 36.2 jit_solution(7349933937296641670)
XLA Ops:
  0.0 33.6 %bands.1.band_ref = bf16[256,128]{1,0:T(8,128)(2,1)} custom-call(bf16[10240,1024]{1,0:T(8,128)(2,1)} %bitcast.6, bf16[1024,256]{1,0:T(8,128)(2,1)} %constant.10.table_hbm, bf16[4,256,512]{2,1,0:T(8,128)(2,1)} %bitcast.7, bf16[4,512,256]{2,1,0:T(8,128)(2,1)} %bitcast.8, s32[2,40]{1,0:T(2,128)} %bitcast.9, s32[2,40]{1,0:T(2,128)} %bitcast.10), custom_call_target="tpu_custom_call" | custom-call | tf_op jit(solution)/shard_map/bands/pallas_call | solution.py:441
  33.6 2.6 %series.1 = bf16[4,8,32,1024]{3,2,1,0:T(8,128)(2,1)} custom-call(bf16[256,128]{1,0:T(8,128)(2,1)} %bands.1.band_ref, bf16[32,1024]{1,0:T(8,128)(2,1)} %constant.11.table_ref), custom_call_target="tpu_custom_call" | custom-call | tf_op jit(solution)/shard_map/series/pallas_call | solution.py:477

commit v2 on v1

--- a/solution.py
+++ b/solution.py
@@ -131,8 +131,8 @@
 
 def band_kernel(
     groups, chunks, tile, src_dev,
-    wave, table_hbm, u_hbm, v_hbm, starts_hbm, counts_hbm, out_ref,
-    starts, counts, table, u_ref, v_ref, owner, wbuf, spec, send, xbuf, acc, bsend, brecv,
+    wave, table_hbm, u_hbm, v_hbm, starts_hbm, counts_hbm, out_hbm,
+    starts, counts, table, u_ref, v_ref, owner, wbuf, spec, send, xbuf, acc, bsend,
     isem, tsem, usem, vsem, wsem, sa, ra, sx, rx, sf, rv, ru, ro, sb, rb,
 ):
     me = lax.axis_index("freq")
@@ -142,7 +142,10 @@
     across = lax.rem(row + 2, 4)
     partner = row + 1 - 2 * core
     half = groups // 2
+    quarter = groups // 4
     own_half = me // half
+    place = me // quarter
+    edge = 1 + (place * place - 3 * place) // 2
     steps = 2 * chunks
     width = tile // 2
     freq_dev = owner.shape[1]
@@ -265,7 +268,7 @@
             exchange(h, peer, me, ra.at[h, 0]).start()
         for d in range(half):
             peer = (1 - own_half) * half + lax.rem(me + d, half)
-            exchange(h, peer, me, ra.at[h, 1]).start()
+            exchange(h, peer, me, ra.at[h, 1 + edge]).start()
 
     def relay_near(h):
         pltpu.make_async_copy(
@@ -274,11 +277,17 @@
         for d in range(1, half):
             cross(h, own_half * half + lax.rem(me + d, half), 1, side).start()
 
-    def relay_far(h):
-        pltpu.make_async_copy(
-            xbuf.at[h, side, pl.ds(0, half)], xbuf.at[h, side, pl.ds(0, half)], ra.at[h, 1]
-        ).wait()
-        cross(h, (1 - own_half) * half, half, side).start()
+    def relay_far(h, outer):
+        first = (1 - own_half) * 3 * quarter if outer else (2 - own_half) * quarter
+        block = xbuf.at[h, side, pl.ds(first, quarter)]
+        pltpu.make_async_copy(block, block, ra.at[h, 1 + outer]).wait()
+        cross(h, first, quarter, side).start()
+
+    def relay_inner(h):
+        relay_far(h, 0)
+
+    def relay_outer(h):
+        relay_far(h, 1)
 
     def project(c):
         for n in range(2):
@@ -311,8 +320,8 @@
         pl.when((h >= 2) & (h < 2 + factors))(lambda: share_v(h - 2).start())
         pl.when((h >= 2 + factors) & (h < 2 + 2 * factors))(lambda: share_u(h - 2 - factors).start())
         pl.when(h >= LAG)(lambda: relay_near(h - LAG))
-        pl.when(h == LAG + 2)(lambda: relay_far(0))
-        pl.when(h > 2 * LAG)(lambda: relay_far(h - 2 * LAG))
+        pl.when(h > LAG)(lambda: relay_outer(h - LAG - 1))
+        pl.when((h > LAG + 1) & (lax.rem(h, 2) == 1))(lambda: relay_inner((h - LAG - 2) // 2))
         return carry
 
     load_table.wait()
@@ -321,17 +330,26 @@
     to_partner(v_ref.at[0], v_ref.at[1], rv).wait_recv()
     share_owner.wait_recv()
 
-    near_turn = {steps - LAG + n: n for n in range(LAG)}
-    far_turn = {}
-    for c in range(chunks):
-        for h in range(steps - 2 * LAG, min(steps, max(2 * c + 4, steps + 1 - 2 * LAG + c))):
-            far_turn.setdefault(h, c)
+    early = (steps - LAG - 1) // 2
+    order = [("inner", early), ("near", steps - 3), ("outer", steps - 4)]
+    order += [("near", steps - 2), ("project", 0), ("outer", steps - 3)]
+    order += [("inner", early + 1), ("near", steps - 1), ("outer", steps - 2)]
+    order += [("inner", early + 2), ("outer", steps - 1), ("inner", early + 3), ("project", 1)]
+    order += [("inner", h) for h in range(early + 4, steps)]
+    order += [("project", c) for c in range(2, chunks)]
+    turns, turn = [], []
+    for kind, n in order:
+        if kind == "project":
+            turns.append(turn)
+            turn = []
+        else:
+            turn.append((kind, n))
+    relays = {"near": relay_near, "inner": relay_inner, "outer": relay_outer}
 
     def second_pass(c, carry):
-        for h, turn in far_turn.items():
-            pl.when(c == turn)(functools.partial(relay_far, h))
-        for h, turn in near_turn.items():
-            pl.when(c == turn)(functools.partial(relay_near, h))
+        for n, turn in enumerate(turns):
+            if turn:
+                pl.when(c == n)(lambda turn=turn: [relays[kind](h) for kind, h in turn] and None)
         project(c)
         return carry
 
@@ -343,7 +361,7 @@
     def give_back(i, peer):
         return pltpu.make_async_remote_copy(
             src_ref=bsend.at[i, peer],
-            dst_ref=brecv.at[core * groups + me],
+            dst_ref=out_hbm.at[core * groups + me],
             send_sem=sb,
             recv_sem=rb,
             device_id=(peer, partner if i else row),
@@ -379,7 +397,8 @@
         return carry
 
     lax.fori_loop(0, groups, start_back, 0)
-    brecv[core * groups + me] = bsend[0, me]
+    keep = pltpu.make_async_copy(bsend.at[0, me], out_hbm.at[core * groups + me], isem.at[0])
+    keep.start()
 
     sent = send.at[:, pl.ds(0, (groups - 1) * piece)]
     pltpu.make_async_copy(sent, sent, sa).wait()
@@ -387,10 +406,10 @@
     pltpu.make_async_copy(v_ref.at[0], v_ref.at[0], sf).wait()
     pltpu.make_async_copy(u_ref.at[0], u_ref.at[0], sf).wait()
     pltpu.make_async_copy(owner.at[0], owner.at[0], sf).wait()
-    arrived = brecv.at[pl.ds(0, 2 * groups - 1)]
+    arrived = out_hbm.at[pl.ds(0, 2 * groups - 1)]
+    keep.wait()
     pltpu.make_async_copy(arrived, arrived, sb).wait()
     pltpu.make_async_copy(arrived, arrived, rb).wait()
-    out_ref[...] = brecv[...].reshape(out_ref.shape)
 
 
 def series_kernel(band_ref, table_ref, out_hbm, wide, out, sem):
@@ -440,9 +459,9 @@
     dma = pltpu.SemaphoreType.DMA
     bands = pl.pallas_call(
         functools.partial(band_kernel, groups, chunks, tile, src_dev),
-        out_shape=jax.ShapeDtypeStruct((2 * groups * band_rows, LANES), jnp.bfloat16),
+        out_shape=jax.ShapeDtypeStruct((2 * groups, band_rows, LANES), jnp.bfloat16),
         in_specs=[hbm] * 6,
-        out_specs=vmem,
+        out_specs=hbm,
         scratch_shapes=[
             pltpu.SMEM(tile_offsets[:, 0].shape, jnp.int32),
             pltpu.SMEM(tile_ranks[:, 0].shape, jnp.int32),
@@ -456,9 +475,8 @@
             pltpu.VMEM((steps, 2, groups, piece, width), jnp.bfloat16),
             pltpu.VMEM((2, freq_dev, 2, 2, 2 * src_dev, slots), jnp.float32),
             pltpu.VMEM((2, groups, band_rows, LANES), jnp.bfloat16),
-            pltpu.VMEM((2 * groups, band_rows, LANES), jnp.bfloat16),
             dma((2,)), dma, dma, dma, dma((steps,)),
-            dma, dma((steps, 2)), dma, dma((steps,)),
+            dma, dma((steps, 3)), dma, dma((steps,)),
             dma, dma, dma, dma, dma, dma,
         ],
         compiler_params=pltpu.CompilerParams(
@@ -472,7 +490,7 @@
         v_factors.reshape(factors, slots, tile),
         tile_offsets[:, 0],
         tile_ranks[:, 0],
-    )
+    ).reshape(2 * groups * band_rows, LANES)
     shape = (q_low, q_high, sources, samples)
     series = pl.pallas_call(
         series_kernel,

time: 36.3 us -> 34.9 us (0.961)
  Pallas kernels: 36.2 us -> 34.7 us
    pallas_call x1, Pallas kernels: 33.6 us -> 32.2 us  [fast_device(): pl.pallas_call(functools.partial(band_kernel, groups, chunks, tile, src_d...]
where the time goes in v2:
time: 34.9 us; the launch traced here: 34.8 us
  Pallas kernels  34.7 us (99%)
    pallas_call x1, Pallas kernels, fast_device(): pl.pallas_call(functools.partial(band_kernel, groups, chunks, tile, src_d...  32.2 us
    pallas_call x1, Pallas kernels, fast_device(): pl.pallas_call(series_kernel, out_shape=jax.ShapeDtypeStruct(shape, jnp.b...  2.55 us

profile of v2, /device:TPU:0, one launch (start us, length us, event | category | flops | bytes accessed | tf_op | source)
XLA Modules:
  0.0 34.8 jit_solution(4808098657116092372)
XLA Ops:
  0.0 32.2 %bands.1 = bf16[16,16,128]{2,1,0:T(8,128)(2,1)} custom-call(bf16[10240,1024]{1,0:T(8,128)(2,1)} %bitcast.7, bf16[1024,256]{1,0:T(8,128)(2,1)} %constant.10.table_hbm, bf16[4,256,512]{2,1,0:T(8,128)(2,1)} %bitcast.8, bf16[4,512,256]{2,1,0:T(8,128)(2,1)} %bitcast.9, s32[2,40]{1,0:T(2,128)} %bitcast.11, s32[2,40]{1,0:T(2,128)} %bitcast.12), custom_call_target="tpu_custom_call" | custom-call | tf_op jit(solution)/shard_map/bands/pallas_call | solution.py:460
  32.2 2.6 %series.1 = bf16[4,8,32,1024]{3,2,1,0:T(8,128)(2,1)} custom-call(bf16[256,128]{1,0:T(8,128)(2,1)} %bitcast.10, bf16[32,1024]{1,0:T(8,128)(2,1)} %constant.11.table_ref), custom_call_target="tpu_custom_call" | custom-call | tf_op jit(solution)/shard_map/series/pallas_call | solution.py:495

commit v3 on v2

--- a/solution.py
+++ b/solution.py
@@ -13,6 +13,8 @@
 MESH = pl.DeviceIdType.MESH
 LANES = 128
 LAG = 3
+DIRECT = 3
+OLAG = 5
 
 
 def spectral_tables(freq_count, sample_count):
@@ -150,7 +152,9 @@
     width = tile // 2
     freq_dev = owner.shape[1]
     slots = owner.shape[3]
-    piece = send.shape[1] // groups
+    rows = 2 * src_dev
+    outer_first = (1 - own_half) * 3 * quarter
+    inner_first = (2 - own_half) * quarter
     factors = u_ref.shape[1]
     step_rows = width * src_dev
 
@@ -178,7 +182,9 @@
         return carry
 
     lax.fori_loop(1, groups, greet, 0)
-    pl.semaphore_signal(barrier, inc=1, device_id=(me, across), device_id_type=MESH)
+    for d in range(half):
+        peer = own_half * half + lax.rem(me + d, half)
+        pl.semaphore_signal(barrier, inc=1, device_id=(peer, across), device_id_type=MESH)
     pl.semaphore_signal(barrier, inc=1, device_id=(me, partner), device_id_type=MESH)
 
     def start_load(h, carry):
@@ -206,7 +212,7 @@
 
     def exchange(h, peer, sender, r_sem):
         return pltpu.make_async_remote_copy(
-            src_ref=send.at[h, pl.ds(peer * piece, piece)],
+            src_ref=send.at[h, peer],
             dst_ref=xbuf.at[h, side, sender],
             send_sem=sa,
             recv_sem=r_sem,
@@ -219,7 +225,7 @@
             src_ref=xbuf.at[h, block, pl.ds(first, count)],
             dst_ref=xbuf.at[h, block, pl.ds(first, count)],
             send_sem=sx,
-            recv_sem=rx.at[h],
+            recv_sem=rx.at[h // 2],
             device_id=(me, across),
             device_id_type=MESH,
         )
@@ -251,34 +257,45 @@
         for p in range(spec.shape[0]):
             spec[p] = values[:, p * LANES : (p + 1) * LANES]
         for p in range(spec.shape[0]):
-            cols = slice(p * LANES, (p + 1) * LANES)
             picked = spec[p, pl.ds(0, width, stride=src_dev), :]
             for s in range(1, src_dev):
                 picked = jnp.where(
                     lane_mod == s, spec[p, pl.ds(s, width, stride=src_dev), :], picked
                 )
-            send[h, cols, :] = picked.T.astype(jnp.bfloat16)
-        own = pl.multiple_of(me * piece, piece)
-        xbuf[h, side, me] = send[h, pl.ds(own, piece), :]
+            turned = picked.T.astype(jnp.bfloat16).reshape(-1, freq_dev, rows, width)
+            peers = slice(p * turned.shape[0], (p + 1) * turned.shape[0])
+            send[h, peers] = turned
+        xbuf[h, side, me] = send[h, me]
+
+    def direct(h, peer):
+        return pltpu.make_async_remote_copy(
+            src_ref=send.at[h, peer],
+            dst_ref=xbuf.at[h, side, me],
+            send_sem=sx,
+            recv_sem=rx.at[h // 2],
+            device_id=(peer, across),
+            device_id_type=MESH,
+        )
 
     def distribute(h):
         cross(h, me, 1, side).start()
-        for d in range(1, half):
-            peer = own_half * half + lax.rem(me + d, half)
+        near = [own_half * half + lax.rem(me + d, half) for d in range(1, half)]
+        for peer in near:
             exchange(h, peer, me, ra.at[h, 0]).start()
         for d in range(half):
             peer = (1 - own_half) * half + lax.rem(me + d, half)
             exchange(h, peer, me, ra.at[h, 1 + edge]).start()
+        pl.when(h < DIRECT)(lambda: [direct(h, peer).start() for peer in near] and None)
 
     def relay_near(h):
         pltpu.make_async_copy(
             xbuf.at[h, side, pl.ds(0, half - 1)], xbuf.at[h, side, pl.ds(0, half - 1)], ra.at[h, 0]
         ).wait()
-        for d in range(1, half):
-            cross(h, own_half * half + lax.rem(me + d, half), 1, side).start()
+        near = [own_half * half + lax.rem(me + d, half) for d in range(1, half)]
+        pl.when(h >= DIRECT)(lambda: [cross(h, peer, 1, side).start() for peer in near] and None)
 
     def relay_far(h, outer):
-        first = (1 - own_half) * 3 * quarter if outer else (2 - own_half) * quarter
+        first = outer_first if outer else inner_first
         block = xbuf.at[h, side, pl.ds(first, quarter)]
         pltpu.make_async_copy(block, block, ra.at[h, 1 + outer]).wait()
         cross(h, first, quarter, side).start()
@@ -289,38 +306,37 @@
     def relay_outer(h):
         relay_far(h, 1)
 
+    def crossed(c):
+        block = xbuf.at[pl.ds(0, 2), 1 - side]
+        pltpu.make_async_copy(block, block, rx.at[c]).wait()
+
     def project(c):
-        for n in range(2):
-            cross(2 * c + n, 0, groups, 1 - side).wait_recv()
-        rows = 2 * src_dev
+        crossed(c)
         for k in range(freq_dev):
-            parts = [
-                xbuf[2 * c + n, :, :, k * rows : (k + 1) * rows, :].reshape(2 * groups * rows, width)
-                for n in range(2)
-            ]
-            left = jnp.concatenate(parts, axis=1)
+            halves = [xbuf[2 * c + n, :, :, k].reshape(2 * groups * rows, width) for n in range(2)]
+            left = jnp.concatenate(halves, axis=1)
             for i in range(2):
                 held = owner[i, k]
-                inside = [(held == g * chunks + c)[0:1] for g in range(groups)]
+                inside = [(held == g * chunks + c)[None, None] for g in range(groups)]
                 for a in range(2):
                     products = lax.dot_general(
                         left, v_ref[i, a * freq_dev + k], (((1,), (1,)), ((), ())),
                         preferred_element_type=jnp.float32,
-                    ).reshape(2, groups, rows, slots)
-                    total = acc[i, k, a]
+                    ).reshape(2, groups, 2, src_dev, slots)
+                    total = acc[i, k, a].reshape(2, 2, src_dev, slots)
                     for g in range(groups):
-                        total = jnp.where(inside[g][None], products[:, g], total)
-                    acc[i, k, a] = total
+                        total = jnp.where(inside[g], products[:, g], total)
+                    acc[i, k, a] = total.reshape(2, rows, slots)
 
     def first_pass(h, carry):
         transform(h)
-        pl.when(h == 0)(lambda: pl.semaphore_wait(barrier, 2 * groups))
+        pl.when(h == 0)(lambda: pl.semaphore_wait(barrier, 2 * groups + half - 1))
         distribute(h)
         pl.when(h == 1)(share_owner.start)
         pl.when((h >= 2) & (h < 2 + factors))(lambda: share_v(h - 2).start())
         pl.when((h >= 2 + factors) & (h < 2 + 2 * factors))(lambda: share_u(h - 2 - factors).start())
         pl.when(h >= LAG)(lambda: relay_near(h - LAG))
-        pl.when(h > LAG)(lambda: relay_outer(h - LAG - 1))
+        pl.when(h >= OLAG)(lambda: relay_outer(h - OLAG))
         pl.when((h > LAG + 1) & (lax.rem(h, 2) == 1))(lambda: relay_inner((h - LAG - 2) // 2))
         return carry
 
@@ -330,12 +346,12 @@
     to_partner(v_ref.at[0], v_ref.at[1], rv).wait_recv()
     share_owner.wait_recv()
 
-    early = (steps - LAG - 1) // 2
-    order = [("inner", early), ("near", steps - 3), ("outer", steps - 4)]
-    order += [("near", steps - 2), ("project", 0), ("outer", steps - 3)]
-    order += [("inner", early + 1), ("near", steps - 1), ("outer", steps - 2)]
-    order += [("inner", early + 2), ("outer", steps - 1), ("inner", early + 3), ("project", 1)]
-    order += [("inner", h) for h in range(early + 4, steps)]
+    late = (steps - LAG - 1) // 2
+    order = [("inner", late), ("near", steps - 3), ("outer", steps - 5), ("outer", steps - 4)]
+    order += [("project", 0), ("outer", steps - 3), ("inner", late + 1), ("near", steps - 2)]
+    order += [("outer", steps - 2), ("inner", late + 2), ("inner", late + 3), ("project", 1)]
+    order += [("inner", late + 4), ("near", steps - 1), ("outer", steps - 1)]
+    order += [("inner", h) for h in range(late + 5, steps)]
     order += [("project", c) for c in range(2, chunks)]
     turns, turn = [], []
     for kind, n in order:
@@ -346,10 +362,13 @@
             turn.append((kind, n))
     relays = {"near": relay_near, "inner": relay_inner, "outer": relay_outer}
 
-    def second_pass(c, carry):
+    def relay_turn(c):
         for n, turn in enumerate(turns):
             if turn:
                 pl.when(c == n)(lambda turn=turn: [relays[kind](h) for kind, h in turn] and None)
+
+    def second_pass(c, carry):
+        relay_turn(c)
         project(c)
         return carry
 
@@ -364,21 +383,19 @@
             dst_ref=out_hbm.at[core * groups + me],
             send_sem=sb,
             recv_sem=rb,
-            device_id=(peer, partner if i else row),
+            device_id=(peer, row + i * (partner - row)),
             device_id_type=MESH,
         )
 
     contract = (((1,), (1,)), ((), ()))
-    sources = 2 * src_dev
-    q_low = LANES // (2 * sources)
+    q_low = LANES // (2 * rows)
     q_high = tile // groups // q_low
-    for i in (1, 0):
-        rows_out = []
+    for i in (core, 1 - core):
         for k in range(freq_dev):
             first = acc[i, k, 0].reshape(2, 2, src_dev, slots)
             second = acc[i, k, 1].reshape(2, 2, src_dev, slots)
-            real = (first[:, 0] - second[:, 1]).reshape(sources, slots)
-            imag = (first[:, 1] + second[:, 0]).reshape(sources, slots)
+            real = (first[:, 0] - second[:, 1]).reshape(rows, slots)
+            imag = (first[:, 1] + second[:, 0]).reshape(rows, slots)
             straight = jnp.concatenate([real, imag], axis=0).astype(jnp.bfloat16)
             turned = jnp.concatenate([-imag, real], axis=0).astype(jnp.bfloat16)
             band = lax.dot_general(
@@ -387,29 +404,29 @@
             band = band + lax.dot_general(
                 u_ref[i, freq_dev + k], turned, contract, preferred_element_type=jnp.float32
             )
-            split = band.reshape(groups, q_low, q_high, 2 * sources)
-            rows_out.append(jnp.concatenate([split[:, q] for q in range(q_low)], axis=-1))
-        bsend[i] = jnp.concatenate(rows_out, axis=1).astype(jnp.bfloat16)
-
-    def start_back(d, carry):
-        give_back(1, lax.rem(me + groups // 2 + d, groups)).start()
-        pl.when(d != groups // 2)(lambda: give_back(0, lax.rem(me + groups // 2 + d, groups)).start())
-        return carry
-
-    lax.fori_loop(0, groups, start_back, 0)
+            parts = band.reshape(groups, q_low, q_high, 2 * rows)
+            parts = jnp.concatenate([parts[:, q] for q in range(q_low)], axis=-1)
+            bsend[i, :, k] = parts.astype(jnp.bfloat16)
+
+        def start_back(d, carry, i=i):
+            peer = (1 - own_half) * (groups - 1) + (2 * own_half - 1) * d
+            pl.when((i == 1) | (peer != me))(lambda: give_back(i, peer).start())
+            return carry
+
+        lax.fori_loop(0, groups, start_back, 0)
     keep = pltpu.make_async_copy(bsend.at[0, me], out_hbm.at[core * groups + me], isem.at[0])
     keep.start()
 
-    sent = send.at[:, pl.ds(0, (groups - 1) * piece)]
+    sent = send.at[:, pl.ds(0, groups - 1)]
     pltpu.make_async_copy(sent, sent, sa).wait()
     pltpu.make_async_copy(xbuf.at[:, 0], xbuf.at[:, 0], sx).wait()
     pltpu.make_async_copy(v_ref.at[0], v_ref.at[0], sf).wait()
     pltpu.make_async_copy(u_ref.at[0], u_ref.at[0], sf).wait()
     pltpu.make_async_copy(owner.at[0], owner.at[0], sf).wait()
-    arrived = out_hbm.at[pl.ds(0, 2 * groups - 1)]
     keep.wait()
-    pltpu.make_async_copy(arrived, arrived, sb).wait()
-    pltpu.make_async_copy(arrived, arrived, rb).wait()
+    back = out_hbm.at[pl.ds(0, 2 * groups - 1)]
+    pltpu.make_async_copy(back, back, sb).wait()
+    pltpu.make_async_copy(back, back, rb).wait()
 
 
 def series_kernel(band_ref, table_ref, out_hbm, wide, out, sem):
@@ -447,19 +464,17 @@
     inverse = inverse.reshape(freqs, 2, samples).transpose(1, 0, 2).reshape(2 * freqs, samples)
     inverse = jnp.asarray(inverse).astype(jnp.bfloat16)
     columns = table.shape[1]
-    piece = columns // groups
     sources = 4 * src_dev
     q_dev = tile // groups
     q_low = LANES // sources
     q_high = q_dev // q_low
-    band_rows = freq_dev * q_high
     factors = 2 * freq_dev
     vmem = pl.BlockSpec(memory_space=pltpu.VMEM)
     hbm = pl.BlockSpec(memory_space=pl.ANY)
     dma = pltpu.SemaphoreType.DMA
     bands = pl.pallas_call(
         functools.partial(band_kernel, groups, chunks, tile, src_dev),
-        out_shape=jax.ShapeDtypeStruct((2 * groups, band_rows, LANES), jnp.bfloat16),
+        out_shape=jax.ShapeDtypeStruct((2 * groups, freq_dev, q_high, LANES), jnp.bfloat16),
         in_specs=[hbm] * 6,
         out_specs=hbm,
         scratch_shapes=[
@@ -471,12 +486,12 @@
             pltpu.VMEM((2, freq_dev, 8, slots), jnp.int32),
             pltpu.VMEM((steps, width * src_dev, samples), jnp.bfloat16),
             pltpu.VMEM((columns // LANES, width * src_dev, LANES), jnp.float32),
-            pltpu.VMEM((steps, columns, width), jnp.bfloat16),
-            pltpu.VMEM((steps, 2, groups, piece, width), jnp.bfloat16),
+            pltpu.VMEM((steps, groups, freq_dev, 2 * src_dev, width), jnp.bfloat16),
+            pltpu.VMEM((steps, 2, groups, freq_dev, 2 * src_dev, width), jnp.bfloat16),
             pltpu.VMEM((2, freq_dev, 2, 2, 2 * src_dev, slots), jnp.float32),
-            pltpu.VMEM((2, groups, band_rows, LANES), jnp.bfloat16),
+            pltpu.VMEM((2, groups, freq_dev, q_high, LANES), jnp.bfloat16),
             dma((2,)), dma, dma, dma, dma((steps,)),
-            dma, dma((steps, 3)), dma, dma((steps,)),
+            dma, dma((steps, 3)), dma, dma((chunks,)),
             dma, dma, dma, dma, dma, dma,
         ],
         compiler_params=pltpu.CompilerParams(
@@ -490,7 +505,7 @@
         v_factors.reshape(factors, slots, tile),
         tile_offsets[:, 0],
         tile_ranks[:, 0],
-    ).reshape(2 * groups * band_rows, LANES)
+    ).reshape(2 * groups * freq_dev * q_high, LANES)
     shape = (q_low, q_high, sources, samples)
     series = pl.pallas_call(
         series_kernel,
@@ -515,7 +530,7 @@
     aligned = aligned and samples % LANES == 0
     counts = u_factors.shape[1] == 2 and u_factors.shape[2] == 1 and src_dev == 8
     counts = counts and lax.axis_size("rows") == 4 and groups % 2 == 0
-    if aligned and counts and tile == groups * 32:
+    if aligned and counts and tile == groups * 32 and rec_dev >= 4 * tile:
         return fast_device(wavefield, u_factors, v_factors, tile_ranks, tile_offsets)
     return general_device(wavefield, u_factors, v_factors, tile_ranks, tile_offsets)
 

time: 34.9 us -> 34.3 us (0.983)
  Pallas kernels: 34.7 us -> 34.1 us
    pallas_call x1, Pallas kernels: 32.2 us -> 31.6 us  [fast_device(): pl.pallas_call(functools.partial(band_kernel, groups, chunks, tile, src_d...]
where the time goes in v3:
time: 34.3 us; the launch traced here: 34.1 us
  Pallas kernels  34.1 us (99%)
    pallas_call x1, Pallas kernels, fast_device(): pl.pallas_call(functools.partial(band_kernel, groups, chunks, tile, src_d...  31.6 us
    pallas_call x1, Pallas kernels, fast_device(): pl.pallas_call(series_kernel, out_shape=jax.ShapeDtypeStruct(shape, jnp.b...  2.55 us

profile of v3, /device:TPU:0, one launch (start us, length us, event | category | flops | bytes accessed | tf_op | source)
XLA Modules:
  0.0 34.1 jit_solution(18303347591972019388)
XLA Ops:
  0.0 31.6 %bands.1 = bf16[16,2,8,128]{3,2,1,0:T(8,128)(2,1)} custom-call(bf16[10240,1024]{1,0:T(8,128)(2,1)} %bitcast.7, bf16[1024,256]{1,0:T(8,128)(2,1)} %constant.10.table_hbm, bf16[4,256,512]{2,1,0:T(8,128)(2,1)} %bitcast.8, bf16[4,512,256]{2,1,0:T(8,128)(2,1)} %bitcast.9, s32[2,40]{1,0:T(2,128)} %bitcast.11, s32[2,40]{1,0:T(2,128)} %bitcast.12), custom_call_target="tpu_custom_call" | custom-call | tf_op jit(solution)/shard_map/bands/pallas_call | solution.py:475
  31.6 2.6 %series.1 = bf16[4,8,32,1024]{3,2,1,0:T(8,128)(2,1)} custom-call(bf16[256,128]{1,0:T(8,128)(2,1)} %bitcast.10, bf16[32,1024]{1,0:T(8,128)(2,1)} %constant.11.table_ref), custom_call_target="tpu_custom_call" | custom-call | tf_op jit(solution)/shard_map/series/pallas_call | solution.py:510

commit v4 on v3

--- a/solution.py
+++ b/solution.py
@@ -158,18 +158,22 @@
     factors = u_ref.shape[1]
     step_rows = width * src_dev
 
-    def load(h):
+    def load(c):
         return pltpu.make_async_copy(
-            wave.at[pl.ds(h * step_rows, step_rows)], wbuf.at[h], wsem.at[h]
-        )
+            wave.at[pl.ds(2 * c, 2)], wbuf.at[pl.ds(2 * c, 2)], wsem.at[c + 1]
+        )
+
+    def load_first(h):
+        return pltpu.make_async_copy(wave.at[h], wbuf.at[h], wsem.at[h])
 
     load_table = pltpu.make_async_copy(table_hbm, table, tsem)
     load_v = pltpu.make_async_copy(v_hbm, v_ref.at[0], vsem)
     load_u = pltpu.make_async_copy(u_hbm, u_ref.at[0], usem)
     load_starts = pltpu.make_async_copy(starts_hbm, starts, isem.at[0])
     load_counts = pltpu.make_async_copy(counts_hbm, counts, isem.at[1])
-    load(0).start()
+    load_first(0).start()
     load_table.start()
+    load_first(1).start()
     load_starts.start()
     load_counts.start()
 
@@ -191,7 +195,7 @@
         load(h).start()
         return carry
 
-    lax.fori_loop(1, steps, start_load, 0)
+    lax.fori_loop(1, chunks, start_load, 0)
     load_v.start()
     load_u.start()
 
@@ -249,7 +253,8 @@
     share_owner = to_partner(owner.at[0], owner.at[1], ro)
 
     def transform(h):
-        load(h).wait()
+        pl.when(h < 2)(lambda: load_first(h).wait())
+        pl.when((h > 1) & (lax.rem(h, 2) == 0))(lambda: load(h // 2).wait())
         values = lax.dot_general(
             wbuf[h], table[...], (((1,), (0,)), ((), ())),
             preferred_element_type=jnp.float32,
@@ -490,7 +495,7 @@
             pltpu.VMEM((steps, 2, groups, freq_dev, 2 * src_dev, width), jnp.bfloat16),
             pltpu.VMEM((2, freq_dev, 2, 2, 2 * src_dev, slots), jnp.float32),
             pltpu.VMEM((2, groups, freq_dev, q_high, LANES), jnp.bfloat16),
-            dma((2,)), dma, dma, dma, dma((steps,)),
+            dma((2,)), dma, dma, dma, dma((chunks + 1,)),
             dma, dma((steps, 3)), dma, dma((chunks,)),
             dma, dma, dma, dma, dma, dma,
         ],
@@ -499,7 +504,7 @@
         ),
         name="bands",
     )(
-        wavefield.reshape(rec_dev * src_dev, samples),
+        wavefield.reshape(steps, width * src_dev, samples),
         table,
         u_factors.reshape(factors, tile, slots),
         v_factors.reshape(factors, slots, tile),

time: 34.3 us -> 34.2 us (level)
  no operation moved by 1% of the time
where the time goes in v4:
time: 34.2 us; the launch traced here: 34.1 us
  Pallas kernels  34.1 us (100%)
    pallas_call x1, Pallas kernels, fast_device(): pl.pallas_call(functools.partial(band_kernel, groups, chunks, tile, src_d...  31.5 us
    pallas_call x1, Pallas kernels, fast_device(): pl.pallas_call(series_kernel, out_shape=jax.ShapeDtypeStruct(shape, jnp.b...  2.55 us

profile of v4, /device:TPU:0, one launch (start us, length us, event | category | flops | bytes accessed | tf_op | source)
XLA Modules:
  0.0 34.1 jit_solution(11122054012871384897)
XLA Ops:
  0.0 31.5 %bands.1 = bf16[16,2,8,128]{3,2,1,0:T(8,128)(2,1)} custom-call(bf16[10,1024,1024]{2,1,0:T(8,128)(2,1)} %bitcast.7, bf16[1024,256]{1,0:T(8,128)(2,1)} %constant.10.table_hbm, bf16[4,256,512]{2,1,0:T(8,128)(2,1)} %bitcast.8, bf16[4,512,256]{2,1,0:T(8,128)(2,1)} %bitcast.9, s32[2,40]{1,0:T(2,128)} %bitcast.11, s32[2,40]{1,0:T(2,128)} %bitcast.12), custom_call_target="tpu_custom_call" | custom-call | tf_op jit(solution)/shard_map/bands/pallas_call | solution.py:480
  31.5 2.5 %series.1 = bf16[4,8,32,1024]{3,2,1,0:T(8,128)(2,1)} custom-call(bf16[256,128]{1,0:T(8,128)(2,1)} %bitcast.10, bf16[32,1024]{1,0:T(8,128)(2,1)} %constant.11.table_ref), custom_call_target="tpu_custom_call" | custom-call | tf_op jit(solution)/shard_map/series/pallas_call | solution.py:515
